TPU v7x, 32 devices: a whole 2x2x4 slice. The times are simulated.
32 devices in a mesh: cohort: 2 (over x), tile: 16 (over z, y, core).
Axes of the slice: x: 2, y: 2, z: 4, core: 2. Of those that a mesh axis runs over, the one named last changes fastest.
Arguments:
- dosage: bfloat16 [512, 8192], P(('cohort', 'tile')), parts along dimension 0, may hold values from 0 to 2
- covars: float32 [512, 16], P(('cohort', 'tile')), parts along dimension 0, may hold values from -12 to 12, as said below
- phenotypes: float32 [512, 1792], P(('cohort', 'tile')), parts along dimension 0, may hold values from -100 to 100
Outputs:
- mean_chi: float32 [3584], P(('cohort', 'tile')), parts along dimension 0
- hit_rate: float32 [3584], P(('cohort', 'tile')), parts along dimension 0
There are 2 independent parts, one for each index of `cohort`. A program takes and returns all parts, laid end to end along the dimension named above; each array names one. Nothing has to cross between parts.
Inputs may be any that keep to these rules, and one draw needn't show every extreme that they name: `covars`: each covariate column has its own mean and spread.
All inputs are finite; a program needn't handle non-finite values.
Results may differ from a plain program's by a relative error of at most 0.003.
Values may be sent and summed in bfloat16 or wider, within the bound.
A program may use at most 64 MiB of HBM per device.

v0:
```python
import jax
import jax.numpy as jnp
from jax import lax
from jax.sharding import PartitionSpec as P


def local(dosage, covars, phenotypes):
    highest = lax.Precision.HIGHEST
    devices = lax.axis_size("tile")
    local_rows = dosage.shape[0]
    variants = dosage.shape[1]
    samples = local_rows * devices
    genes_all = phenotypes.shape[1]
    gene_own = genes_all // devices
    scale_root = jnp.sqrt(jnp.float32(samples))
    covars_all = lax.all_gather(covars, "tile", axis=0, tiled=True)
    dose_all = lax.all_gather(dosage, "tile", axis=0, tiled=True)
    pheno_own = lax.all_to_all(phenotypes, "tile", split_axis=1, concat_axis=0, tiled=True)
    gram = jnp.dot(covars_all.T, covars_all, precision=highest, preferred_element_type=jnp.float32)
    factor = jnp.linalg.cholesky(gram)
    cov_pheno = jnp.dot(
        covars_all.T, pheno_own, precision=highest, preferred_element_type=jnp.float32
    )
    beta_pheno = jax.scipy.linalg.cho_solve((factor, True), cov_pheno)
    pheno_resid = pheno_own - jnp.dot(
        covars_all, beta_pheno, precision=highest, preferred_element_type=jnp.float32
    )
    pheno_sumsq = jnp.sum(pheno_resid * pheno_resid, axis=0)
    pheno_bf = pheno_resid.astype(jnp.bfloat16)
    pheno_var = pheno_sumsq / samples + 0.1
    width = 1024
    blocks = variants // width

    def one_block(index, totals):
        start = index * width
        dose_block = lax.dynamic_slice_in_dim(dose_all, start, width, 1).astype(jnp.float32)
        cov_dose = jnp.dot(
            covars_all.T, dose_block, precision=highest, preferred_element_type=jnp.float32
        )
        beta_dose = jax.scipy.linalg.cho_solve((factor, True), cov_dose)
        dose_resid = dose_block - jnp.dot(
            covars_all, beta_dose, precision=highest, preferred_element_type=jnp.float32
        )
        dose_var = jnp.sum(dose_resid * dose_resid, axis=0) / samples + 0.1
        cross = lax.dot_general(
            pheno_bf,
            dose_resid.astype(jnp.bfloat16),
            (((0,), (0,)), ((), ())),
            preferred_element_type=jnp.float32,
        )
        zscore = cross / (scale_root * jnp.sqrt(pheno_var[:, None] * dose_var[None, :]))
        chi_square = zscore * zscore
        return (
            totals[0] + jnp.sum(chi_square, axis=1),
            totals[1] + jnp.sum(jax.nn.sigmoid(2.0 * (chi_square - 4.0)), axis=1),
        )

    zeros = jnp.zeros((gene_own,), jnp.float32)
    chi_total, hit_total = lax.fori_loop(0, blocks, one_block, (zeros, zeros))
    return (chi_total / variants, 20.0 / variants * hit_total)


def solution(mesh):
    return jax.shard_map(
        local,
        mesh=mesh,
        in_specs=(
            P(("cohort", "tile"), None),
            P(("cohort", "tile"), None),
            P(("cohort", "tile"), None),
        ),
        out_specs=(P(("cohort", "tile")), P(("cohort", "tile"))),
        check_vma=False,
    )
```

profile of v0, /device:TPU:0, one launch (start us, length us, event | category | flops | bytes accessed | tf_op | source)
XLA Modules:
  0.0 117.5 jit_solution(11533161251048784845)
XLA Ops:
  7.2 0.7 all-gather.2.cloned.1.call-update
  7.9 1.0 all_to_all.14
  8.9 0.7 copy.15
  9.6 7.4 %all-to-all-start = ((f32[16,16,112]{2,0,1:T(8,128)}), f32[16,16,112]{2,0,1:T(8,128)S(1)}, u32[]{:S(2)}, u32[]{:S(2)}) async-start(f32[16,16,112]{2,0,1:T(8,128)} %copy.15), calls=%async_computation | async-start | bytes 262144 | tf_op jit(solution)/shard_map/all_to_all | solution.py:18
  17.0 22.7 %all_gather.7 = f32[256,16]{1,0:T(8,128)S(1)} all-gather(f32[16,16]{1,0:T(8,128)} %param.6), channel_id=1, replica_groups=mesh['cohort'=2,'tile'=16] {'tile'}, dimensions={0}, use_global_device_ids=true | all-gather | bytes 17408 | tf_op jit(solution)/shard_map/all_gather | solution.py:16
  39.8 0.4 fusion.20
  40.2 1.5 %cholesky.18 = f32[16,16]{1,0:T(8,128)S(1)} custom-call(f32[16,16]{1,0:T(8,128)S(1)} %fusion.19), custom_call_target="Cholesky" | custom-call | tf_op jit(solution)/shard_map/jit(cholesky)/cholesky | solution.py:20
  41.7 0.6 compare_reduce_fusion
  42.4 0.6 select_bitcast_fusion
  43.0 1.2 %custom-call.24 = f32[1,16,16]{1,2,0:T(8,128)S(1)} custom-call(f32[1,16,16]{2,1,0:T(8,128)S(1)} %get-tuple-element.272), custom_call_target="InvertDiagBlocksLowerTriangular" | custom-call | tf_op jit(solution)/shard_map/jit(_cho_solve)/triangular_solve | solution.py:24
  44.4 0.3 fusion.21
  45.1 0.4 multiply_reduce_fusion.1
  45.6 18.0 %all-gather.2.cloned.1.call-done = bf16[256,8192]{1,0:T(8,128)(2,1)} async-done(((bf16[16,8192]{1,0:T(8,128)(2,1)}), bf16[256,8192]{1,0:T(8,128)(2,1)}) %all-gather.2.cloned.1.call-update) | async-done | bytes 4194320 | tf_op jit(solution)/shard_map/all_gather | solution.py:17
  63.6 46.5 %while.18 = (s32[]{:T(128)}, f32[112]{0:T(128)S(1)}, f32[112]{0:T(128)S(1)}, bf16[256,8192]{1,0:T(8,128)(2,1)}, f32[16,16]{1,0:T(8,128)S(1)}, /*index=5*/f32[256...) while((s32[]{:T(128)}, f32[112]{0:T(128)S(1)}, ...), condition=%wide.region_7.8_spmd.clone, body=%wide.region_3.7_spmd.clone.sunk | while | flops 168249056 | bytes 2605173 | solution.py:59
  63.6 1.4 %fusion.62 = f32[1024,16]{0,1:T(8,128)S(1)} fusion(f32[256,16]{0,1:T(8,128)S(1)} %get-tuple-element.375, bf16[256,8192]{1,0:T(8,128)(2,1)} %get-tuple-element.373, s32[]{:T(128)S(6)} %select_n.19), kind=kOutput, calls=%fused_computation.7.clone.1 | convolution fusion | flops 50331648 | bytes 606212 | tf_op jit(solution)/shard_map/while/body/eval_jaxpr/dot_general | solution.py:37
  65.0 1.2 %custom-call.29 = f32[1,16,16]{1,2,0:T(8,128)S(1)} custom-call(f32[1,16,16]{2,1,0:T(8,128)S(1)} %bitcast_select_fusion.2), custom_call_target="InvertDiagBlocksLowerTriangular" | custom-call | tf_op jit(solution)/shard_map/while/body/eval_jaxpr/jit(_cho_solve)/triangular_solve | solution.py:40
  66.2 0.3 fusion.63
  66.7 2.1 %multiply_reduce_fusion.3 = (f32[1024]{0:T(1024)S(1)}, bf16[256,1024]{1,0:T(8,128)(2,1)S(1)}) fusion(f32[16,1024]{1,0:T(8,128)S(1)} %fusion.64, f32[256,16]{0,1:T(8,128)S(1)} %get-tuple-element.375, bf16[256,8192]{1,0:T(8,128)(2,1)} %get-tuple-element.373, s32[]{:T(128)S(6)} %select_n.19), kind=kOutput, calls=%fused_computation.5.clone.1 | convolution fusion | flops 51641344 | bytes 1134596 | tf_op jit(solution)/shard_map/while/body/eval_jaxpr/dot_general | solution.py:41
  68.8 0.6 fusion.65
  69.4 1.4 %fusion.62 = f32[1024,16]{0,1:T(8,128)S(1)} fusion(f32[256,16]{0,1:T(8,128)S(1)} %get-tuple-element.375, bf16[256,8192]{1,0:T(8,128)(2,1)} %get-tuple-element.373, s32[]{:T(128)S(6)} %select_n.19), kind=kOutput, calls=%fused_computation.7.clone.1 | convolution fusion | flops 50331648 | bytes 606212 | tf_op jit(solution)/shard_map/while/body/eval_jaxpr/dot_general | solution.py:37
  70.8 1.2 %custom-call.29 = f32[1,16,16]{1,2,0:T(8,128)S(1)} custom-call(f32[1,16,16]{2,1,0:T(8,128)S(1)} %bitcast_select_fusion.2), custom_call_target="InvertDiagBlocksLowerTriangular" | custom-call | tf_op jit(solution)/shard_map/while/body/eval_jaxpr/jit(_cho_solve)/triangular_solve | solution.py:40
  72.5 2.1 %multiply_reduce_fusion.3 = (f32[1024]{0:T(1024)S(1)}, bf16[256,1024]{1,0:T(8,128)(2,1)S(1)}) fusion(f32[16,1024]{1,0:T(8,128)S(1)} %fusion.64, f32[256,16]{0,1:T(8,128)S(1)} %get-tuple-element.375, bf16[256,8192]{1,0:T(8,128)(2,1)} %get-tuple-element.373, s32[]{:T(128)S(6)} %select_n.19), kind=kOutput, calls=%fused_computation.5.clone.1 | convolution fusion | flops 51641344 | bytes 1134596 | tf_op jit(solution)/shard_map/while/body/eval_jaxpr/dot_general | solution.py:41
  74.7 0.6 fusion.65
  75.2 1.4 %fusion.62 = f32[1024,16]{0,1:T(8,128)S(1)} fusion(f32[256,16]{0,1:T(8,128)S(1)} %get-tuple-element.375, bf16[256,8192]{1,0:T(8,128)(2,1)} %get-tuple-element.373, s32[]{:T(128)S(6)} %select_n.19), kind=kOutput, calls=%fused_computation.7.clone.1 | convolution fusion | flops 50331648 | bytes 606212 | tf_op jit(solution)/shard_map/while/body/eval_jaxpr/dot_general | solution.py:37
  76.6 1.2 %custom-call.29 = f32[1,16,16]{1,2,0:T(8,128)S(1)} custom-call(f32[1,16,16]{2,1,0:T(8,128)S(1)} %bitcast_select_fusion.2), custom_call_target="InvertDiagBlocksLowerTriangular" | custom-call | tf_op jit(solution)/shard_map/while/body/eval_jaxpr/jit(_cho_solve)/triangular_solve | solution.py:40
  78.3 2.1 %multiply_reduce_fusion.3 = (f32[1024]{0:T(1024)S(1)}, bf16[256,1024]{1,0:T(8,128)(2,1)S(1)}) fusion(f32[16,1024]{1,0:T(8,128)S(1)} %fusion.64, f32[256,16]{0,1:T(8,128)S(1)} %get-tuple-element.375, bf16[256,8192]{1,0:T(8,128)(2,1)} %get-tuple-element.373, s32[]{:T(128)S(6)} %select_n.19), kind=kOutput, calls=%fused_computation.5.clone.1 | convolution fusion | flops 51641344 | bytes 1134596 | tf_op jit(solution)/shard_map/while/body/eval_jaxpr/dot_general | solution.py:41
  80.5 0.6 fusion.65
  81.1 1.4 %fusion.62 = f32[1024,16]{0,1:T(8,128)S(1)} fusion(f32[256,16]{0,1:T(8,128)S(1)} %get-tuple-element.375, bf16[256,8192]{1,0:T(8,128)(2,1)} %get-tuple-element.373, s32[]{:T(128)S(6)} %select_n.19), kind=kOutput, calls=%fused_computation.7.clone.1 | convolution fusion | flops 50331648 | bytes 606212 | tf_op jit(solution)/shard_map/while/body/eval_jaxpr/dot_general | solution.py:37
  82.4 1.2 %custom-call.29 = f32[1,16,16]{1,2,0:T(8,128)S(1)} custom-call(f32[1,16,16]{2,1,0:T(8,128)S(1)} %bitcast_select_fusion.2), custom_call_target="InvertDiagBlocksLowerTriangular" | custom-call | tf_op jit(solution)/shard_map/while/body/eval_jaxpr/jit(_cho_solve)/triangular_solve | solution.py:40
  84.1 2.1 %multiply_reduce_fusion.3 = (f32[1024]{0:T(1024)S(1)}, bf16[256,1024]{1,0:T(8,128)(2,1)S(1)}) fusion(f32[16,1024]{1,0:T(8,128)S(1)} %fusion.64, f32[256,16]{0,1:T(8,128)S(1)} %get-tuple-element.375, bf16[256,8192]{1,0:T(8,128)(2,1)} %get-tuple-element.373, s32[]{:T(128)S(6)} %select_n.19), kind=kOutput, calls=%fused_computation.5.clone.1 | convolution fusion | flops 51641344 | bytes 1134596 | tf_op jit(solution)/shard_map/while/body/eval_jaxpr/dot_general | solution.py:41
  86.3 0.6 fusion.65
  86.9 1.4 %fusion.62 = f32[1024,16]{0,1:T(8,128)S(1)} fusion(f32[256,16]{0,1:T(8,128)S(1)} %get-tuple-element.375, bf16[256,8192]{1,0:T(8,128)(2,1)} %get-tuple-element.373, s32[]{:T(128)S(6)} %select_n.19), kind=kOutput, calls=%fused_computation.7.clone.1 | convolution fusion | flops 50331648 | bytes 606212 | tf_op jit(solution)/shard_map/while/body/eval_jaxpr/dot_general | solution.py:37
  88.2 1.2 %custom-call.29 = f32[1,16,16]{1,2,0:T(8,128)S(1)} custom-call(f32[1,16,16]{2,1,0:T(8,128)S(1)} %bitcast_select_fusion.2), custom_call_target="InvertDiagBlocksLowerTriangular" | custom-call | tf_op jit(solution)/shard_map/while/body/eval_jaxpr/jit(_cho_solve)/triangular_solve | solution.py:40
  90.0 2.1 %multiply_reduce_fusion.3 = (f32[1024]{0:T(1024)S(1)}, bf16[256,1024]{1,0:T(8,128)(2,1)S(1)}) fusion(f32[16,1024]{1,0:T(8,128)S(1)} %fusion.64, f32[256,16]{0,1:T(8,128)S(1)} %get-tuple-element.375, bf16[256,8192]{1,0:T(8,128)(2,1)} %get-tuple-element.373, s32[]{:T(128)S(6)} %select_n.19), kind=kOutput, calls=%fused_computation.5.clone.1 | convolution fusion | flops 51641344 | bytes 1134596 | tf_op jit(solution)/shard_map/while/body/eval_jaxpr/dot_general | solution.py:41
  92.1 0.6 fusion.65
  92.7 1.4 %fusion.62 = f32[1024,16]{0,1:T(8,128)S(1)} fusion(f32[256,16]{0,1:T(8,128)S(1)} %get-tuple-element.375, bf16[256,8192]{1,0:T(8,128)(2,1)} %get-tuple-element.373, s32[]{:T(128)S(6)} %select_n.19), kind=kOutput, calls=%fused_computation.7.clone.1 | convolution fusion | flops 50331648 | bytes 606212 | tf_op jit(solution)/shard_map/while/body/eval_jaxpr/dot_general | solution.py:37
  94.1 1.2 %custom-call.29 = f32[1,16,16]{1,2,0:T(8,128)S(1)} custom-call(f32[1,16,16]{2,1,0:T(8,128)S(1)} %bitcast_select_fusion.2), custom_call_target="InvertDiagBlocksLowerTriangular" | custom-call | tf_op jit(solution)/shard_map/while/body/eval_jaxpr/jit(_cho_solve)/triangular_solve | solution.py:40
  95.8 2.1 %multiply_reduce_fusion.3 = (f32[1024]{0:T(1024)S(1)}, bf16[256,1024]{1,0:T(8,128)(2,1)S(1)}) fusion(f32[16,1024]{1,0:T(8,128)S(1)} %fusion.64, f32[256,16]{0,1:T(8,128)S(1)} %get-tuple-element.375, bf16[256,8192]{1,0:T(8,128)(2,1)} %get-tuple-element.373, s32[]{:T(128)S(6)} %select_n.19), kind=kOutput, calls=%fused_computation.5.clone.1 | convolution fusion | flops 51641344 | bytes 1134596 | tf_op jit(solution)/shard_map/while/body/eval_jaxpr/dot_general | solution.py:41
  97.9 0.6 fusion.65
  98.5 1.4 %fusion.62 = f32[1024,16]{0,1:T(8,128)S(1)} fusion(f32[256,16]{0,1:T(8,128)S(1)} %get-tuple-element.375, bf16[256,8192]{1,0:T(8,128)(2,1)} %get-tuple-element.373, s32[]{:T(128)S(6)} %select_n.19), kind=kOutput, calls=%fused_computation.7.clone.1 | convolution fusion | flops 50331648 | bytes 606212 | tf_op jit(solution)/shard_map/while/body/eval_jaxpr/dot_general | solution.py:37
  99.9 1.2 %custom-call.29 = f32[1,16,16]{1,2,0:T(8,128)S(1)} custom-call(f32[1,16,16]{2,1,0:T(8,128)S(1)} %bitcast_select_fusion.2), custom_call_target="InvertDiagBlocksLowerTriangular" | custom-call | tf_op jit(solution)/shard_map/while/body/eval_jaxpr/jit(_cho_solve)/triangular_solve | solution.py:40
  101.6 2.1 %multiply_reduce_fusion.3 = (f32[1024]{0:T(1024)S(1)}, bf16[256,1024]{1,0:T(8,128)(2,1)S(1)}) fusion(f32[16,1024]{1,0:T(8,128)S(1)} %fusion.64, f32[256,16]{0,1:T(8,128)S(1)} %get-tuple-element.375, bf16[256,8192]{1,0:T(8,128)(2,1)} %get-tuple-element.373, s32[]{:T(128)S(6)} %select_n.19), kind=kOutput, calls=%fused_computation.5.clone.1 | convolution fusion | flops 51641344 | bytes 1134596 | tf_op jit(solution)/shard_map/while/body/eval_jaxpr/dot_general | solution.py:41
  103.7 0.6 fusion.65
  104.3 1.4 %fusion.62 = f32[1024,16]{0,1:T(8,128)S(1)} fusion(f32[256,16]{0,1:T(8,128)S(1)} %get-tuple-element.375, bf16[256,8192]{1,0:T(8,128)(2,1)} %get-tuple-element.373, s32[]{:T(128)S(6)} %select_n.19), kind=kOutput, calls=%fused_computation.7.clone.1 | convolution fusion | flops 50331648 | bytes 606212 | tf_op jit(solution)/shard_map/while/body/eval_jaxpr/dot_general | solution.py:37
  105.7 1.2 %custom-call.29 = f32[1,16,16]{1,2,0:T(8,128)S(1)} custom-call(f32[1,16,16]{2,1,0:T(8,128)S(1)} %bitcast_select_fusion.2), custom_call_target="InvertDiagBlocksLowerTriangular" | custom-call | tf_op jit(solution)/shard_map/while/body/eval_jaxpr/jit(_cho_solve)/triangular_solve | solution.py:40
  107.4 2.1 %multiply_reduce_fusion.3 = (f32[1024]{0:T(1024)S(1)}, bf16[256,1024]{1,0:T(8,128)(2,1)S(1)}) fusion(f32[16,1024]{1,0:T(8,128)S(1)} %fusion.64, f32[256,16]{0,1:T(8,128)S(1)} %get-tuple-element.375, bf16[256,8192]{1,0:T(8,128)(2,1)} %get-tuple-element.373, s32[]{:T(128)S(6)} %select_n.19), kind=kOutput, calls=%fused_computation.5.clone.1 | convolution fusion | flops 51641344 | bytes 1134596 | tf_op jit(solution)/shard_map/while/body/eval_jaxpr/dot_general | solution.py:41
  109.5 0.6 fusion.65
  110.1 0.5 broadcast_multiply_fusion
  (52 shorter events, 4.4 us)
Async XLA Ops:
  7.2 56.5 %all-gather.2.cloned.1.call-start = ((), (), s32[]{:S(2)}) async-start(), calls=%async_computation.1 | async-start | bytes 4456448 | tf_op jit(solution)/shard_map/all_gather | solution.py:17
  9.6 34.7 %all-to-all-start = ((f32[16,16,112]{2,0,1:T(8,128)}), f32[16,16,112]{2,0,1:T(8,128)S(1)}, u32[]{:S(2)}, u32[]{:S(2)}) async-start(f32[16,16,112]{2,0,1:T(8,128)} %copy.15), calls=%async_computation | async-start | bytes 262144 | tf_op jit(solution)/shard_map/all_to_all | solution.py:18
Sparse Core Ops, SparseCore 0:
  10.1 53.4 all-gather.1
where the time goes:
time: 118 us; the launch traced here: 117 us
  matrix products  37.4 us (32%)
  blocking collectives  22.7 us (19%)
  waiting for transfers between devices  18.7 us (16%)
  other arithmetic  14.6 us (12%)
  between operations  14.1 us (12%)
  starting transfers between devices  7.45 us (6%)
  local copies, waits for them, and re-layouts  2.05 us (2%)
    all_gather x1, blocking collectives, local(): covars_all = lax.all_gather(covars, 'tile', axis=0, tiled=True)  22.7 us
    all_gather x1, waiting for transfers between devices, local(): dose_all = lax.all_gather(dosage, 'tile', axis=0, tiled=True)  18 us
    dot_general x8, matrix products, one_block(): jnp.dot(covars_all, beta_dose, precision=highest, preferred_element_type=...  17 us
    dot_general x8, matrix products, one_block(): jnp.dot(covars_all.T, dose_block, precision=highest, preferred_element_ty...  10.9 us
    another operation x16, other arithmetic, one_block(): beta_dose = jax.scipy.linalg.cho_solve((factor, True), cov_dose)  9.88 us
    all_to_all x1, starting transfers between devices, local(): lax.all_to_all(phenotypes, 'tile', split_axis=1, concat_axis=0, tiled=True)  7.41 us
    dot_general x8, matrix products, one_block(): lax.dot_general(pheno_bf, dose_resid.astype(jnp.bfloat16), (((0,), (0,)),...  4.42 us
    another operation x16, matrix products, one_block(): beta_dose = jax.scipy.linalg.cho_solve((factor, True), cov_dose)  3.7 us
  transfers between devices with their start and end apart: 2, of which 1 were waited for; matrix products, arithmetic and copies ran while one was open for 6% of the time, Pallas kernels for 0%

commit v1 on v0

--- a/solution.py
+++ b/solution.py
@@ -2,6 +2,19 @@
 import jax.numpy as jnp
 from jax import lax
 from jax.sharding import PartitionSpec as P
+
+
+def touch_seats_all_up(field, device_axis):
+    lanes = lax.psum(1, device_axis)
+    rows = list(map(lambda idx: (idx, (idx + 1) % lanes), range(lanes)))
+    u1 = [None] * lanes
+    u1[lanes - 1] = field
+    for num in range(lanes - 2, -1, -1):
+        u1[num] = lax.ppermute(u1[num + 1], device_axis, rows)
+    part_next = jnp.concatenate(u1, axis=0)
+    answer = (lax.axis_index(device_axis) + 1) * field.shape[0]
+    step_out = jnp.roll(part_next, shift=answer, axis=0)
+    return step_out
 
 
 def local(dosage, covars, phenotypes):
@@ -14,7 +27,7 @@
     gene_own = genes_all // devices
     scale_root = jnp.sqrt(jnp.float32(samples))
     covars_all = lax.all_gather(covars, "tile", axis=0, tiled=True)
-    dose_all = lax.all_gather(dosage, "tile", axis=0, tiled=True)
+    dose_all = touch_seats_all_up(dosage, "tile")
     pheno_own = lax.all_to_all(phenotypes, "tile", split_axis=1, concat_axis=0, tiled=True)
     gram = jnp.dot(covars_all.T, covars_all, precision=highest, preferred_element_type=jnp.float32)
     factor = jnp.linalg.cholesky(gram)

time: 118 us -> 211 us (1.79)
  waiting for transfers between devices: 18.7 us -> 114 us
  between operations: 14.1 us -> 0.97 us
  local copies, waits for them, and re-layouts: 2.05 us -> 12.5 us
    ppermute x0 -> x15, waiting for transfers between devices: none -> 114 us  [touch_seats_all_up(): u1[num] = lax.ppermute(u1[num + 1], device_axis, rows)]
    all_gather x1 -> x0, waiting for transfers between devices: 18 us -> none  [local(): dose_all = lax.all_gather(dosage, 'tile', axis=0, tiled=True)]
    unnamed x2 -> x39, local copies, waits for them, and re-layouts: 0.17 us -> 8.39 us
    dynamic_slice x0 -> x1, local copies, waits for them, and re-layouts: none -> 2.23 us  [touch_seats_all_up(): step_out = jnp.roll(part_next, shift=answer, axis=0)]
  transfers between devices with their start and end apart: 2 -> 16, of which waited for: 1 -> 14; matrix products, arithmetic and copies ran while one was open for 6% -> 4% of each run, Pallas kernels for 0% -> 0%
where the time goes in v1:
time: 211 us; the launch traced here: 210 us
  waiting for transfers between devices  114 us (54%)
  matrix products  38.7 us (18%)
  blocking collectives  22.3 us (11%)
  other arithmetic  14.5 us (7%)
  local copies, waits for them, and re-layouts  12.5 us (6%)
  starting transfers between devices  6.76 us (3%)
    ppermute x15, waiting for transfers between devices, touch_seats_all_up(): u1[num] = lax.ppermute(u1[num + 1], device_axis, rows)  114 us
    all_gather x1, blocking collectives, local(): covars_all = lax.all_gather(covars, 'tile', axis=0, tiled=True)  22.3 us
    dot_general x8, matrix products, one_block(): jnp.dot(covars_all, beta_dose, precision=highest, preferred_element_type=...  17 us
    dot_general x8, matrix products, one_block(): jnp.dot(covars_all.T, dose_block, precision=highest, preferred_element_ty...  10.9 us
    another operation x16, other arithmetic, one_block(): beta_dose = jax.scipy.linalg.cho_solve((factor, True), cov_dose)  9.88 us
    unnamed x39, local copies, waits for them, and re-layouts  8.39 us
    all_to_all x1, starting transfers between devices, local(): lax.all_to_all(phenotypes, 'tile', split_axis=1, concat_axis=0, tiled=True)  5.82 us
    dot_general x8, matrix products, one_block(): lax.dot_general(pheno_bf, dose_resid.astype(jnp.bfloat16), (((0,), (0,)),...  4.42 us
  transfers between devices with their start and end apart: 16, of which 14 were waited for; matrix products, arithmetic and copies ran while one was open for 4% of the time, Pallas kernels for 0%

profile of v1, /device:TPU:0, one launch (start us, length us, event | category | flops | bytes accessed | tf_op | source)
XLA Modules:
  0.0 209.9 jit_solution(3852146904921660201)
XLA Ops:
  1.2 9.3 %collective-permute-done = bf16[16,8192]{1,0:T(8,128)(2,1)S(1)} collective-permute-done((bf16[16,8192]{1,0:T(8,128)(2,1)}, bf16[16,8192]{1,0:T(8,128)(2,1)S(1)}, u32[]{:S(2)}, u32[]{:S(2)}) %collective-permute-start) | collective-permute-done | bytes 262176 | tf_op jit(solution)/shard_map/ppermute | solution.py:13
  10.4 8.5 %collective-permute-done.1 = bf16[16,8192]{1,0:T(8,128)(2,1)S(1)} collective-permute-done((bf16[16,8192]{1,0:T(8,128)(2,1)S(1)}, bf16[16,8192]{1,0:T(8,128)(2,1)S(1)}, u32[]{:S(2)}, u32[]{:S(2)}) %collective-permute-start.1) | collective-permute-done | bytes 262176 | tf_op jit(solution)/shard_map/ppermute | solution.py:13
  18.9 8.5 %collective-permute-done.2 = bf16[16,8192]{1,0:T(8,128)(2,1)S(1)} collective-permute-done((bf16[16,8192]{1,0:T(8,128)(2,1)S(1)}, bf16[16,8192]{1,0:T(8,128)(2,1)S(1)}, u32[]{:S(2)}, u32[]{:S(2)}) %collective-permute-start.2) | collective-permute-done | bytes 262176 | tf_op jit(solution)/shard_map/ppermute | solution.py:13
  27.4 8.5 %collective-permute-done.3 = bf16[16,8192]{1,0:T(8,128)(2,1)S(1)} collective-permute-done((bf16[16,8192]{1,0:T(8,128)(2,1)S(1)}, bf16[16,8192]{1,0:T(8,128)(2,1)S(1)}, u32[]{:S(2)}, u32[]{:S(2)}) %collective-permute-start.3) | collective-permute-done | bytes 262176 | tf_op jit(solution)/shard_map/ppermute | solution.py:13
  35.9 8.5 %collective-permute-done.4 = bf16[16,8192]{1,0:T(8,128)(2,1)S(1)} collective-permute-done((bf16[16,8192]{1,0:T(8,128)(2,1)S(1)}, bf16[16,8192]{1,0:T(8,128)(2,1)S(1)}, u32[]{:S(2)}, u32[]{:S(2)}) %collective-permute-start.4) | collective-permute-done | bytes 262176 | tf_op jit(solution)/shard_map/ppermute | solution.py:13
  44.4 8.5 %collective-permute-done.5 = bf16[16,8192]{1,0:T(8,128)(2,1)S(1)} collective-permute-done((bf16[16,8192]{1,0:T(8,128)(2,1)S(1)}, bf16[16,8192]{1,0:T(8,128)(2,1)S(1)}, u32[]{:S(2)}, u32[]{:S(2)}) %collective-permute-start.5) | collective-permute-done | bytes 262176 | tf_op jit(solution)/shard_map/ppermute | solution.py:13
  52.9 8.5 %collective-permute-done.6 = bf16[16,8192]{1,0:T(8,128)(2,1)S(1)} collective-permute-done((bf16[16,8192]{1,0:T(8,128)(2,1)S(1)}, bf16[16,8192]{1,0:T(8,128)(2,1)S(1)}, u32[]{:S(2)}, u32[]{:S(2)}) %collective-permute-start.6) | collective-permute-done | bytes 262176 | tf_op jit(solution)/shard_map/ppermute | solution.py:13
  61.4 8.5 %collective-permute-done.7 = bf16[16,8192]{1,0:T(8,128)(2,1)S(1)} collective-permute-done((bf16[16,8192]{1,0:T(8,128)(2,1)S(1)}, bf16[16,8192]{1,0:T(8,128)(2,1)S(1)}, u32[]{:S(2)}, u32[]{:S(2)}) %collective-permute-start.7) | collective-permute-done | bytes 262176 | tf_op jit(solution)/shard_map/ppermute | solution.py:13
  69.9 8.5 %collective-permute-done.8 = bf16[16,8192]{1,0:T(8,128)(2,1)S(1)} collective-permute-done((bf16[16,8192]{1,0:T(8,128)(2,1)S(1)}, bf16[16,8192]{1,0:T(8,128)(2,1)S(1)}, u32[]{:S(2)}, u32[]{:S(2)}) %collective-permute-start.8) | collective-permute-done | bytes 262176 | tf_op jit(solution)/shard_map/ppermute | solution.py:13
  78.4 8.5 %collective-permute-done.9 = bf16[16,8192]{1,0:T(8,128)(2,1)S(1)} collective-permute-done((bf16[16,8192]{1,0:T(8,128)(2,1)S(1)}, bf16[16,8192]{1,0:T(8,128)(2,1)S(1)}, u32[]{:S(2)}, u32[]{:S(2)}) %collective-permute-start.9) | collective-permute-done | bytes 262176 | tf_op jit(solution)/shard_map/ppermute | solution.py:13
  86.9 1.0 all_to_all.14
  88.6 5.8 %all-to-all-start = ((f32[16,16,112]{2,0,1:T(8,128)}), f32[16,16,112]{2,0,1:T(8,128)S(1)}, u32[]{:S(2)}, u32[]{:S(2)}) async-start(f32[16,16,112]{2,0,1:T(8,128)} %copy.15), calls=%async_computation | async-start | bytes 262144 | tf_op jit(solution)/shard_map/all_to_all | solution.py:31
  94.4 22.3 %all_gather.3 = f32[256,16]{1,0:T(8,128)S(1)} all-gather(f32[16,16]{1,0:T(8,128)} %param.6), channel_id=1, replica_groups=mesh['cohort'=2,'tile'=16] {'tile'}, dimensions={0}, use_global_device_ids=true | all-gather | bytes 17408 | tf_op jit(solution)/shard_map/all_gather | solution.py:29
  117.5 1.4 cholesky.18
  119.6 6.1 %collective-permute-done.11 = bf16[16,8192]{1,0:T(8,128)(2,1)} collective-permute-done((bf16[16,8192]{1,0:T(8,128)(2,1)S(1)}, bf16[16,8192]{1,0:T(8,128)(2,1)}, u32[]{:S(2)}, u32[]{:S(2)}) %collective-permute-start.11) | collective-permute-done | bytes 262176 | tf_op jit(solution)/shard_map/ppermute | solution.py:13
  126.5 1.2 custom-call.24
  128.1 6.5 %collective-permute-done.12 = bf16[16,8192]{1,0:T(8,128)(2,1)} collective-permute-done((bf16[16,8192]{1,0:T(8,128)(2,1)}, bf16[16,8192]{1,0:T(8,128)(2,1)}, u32[]{:S(2)}, u32[]{:S(2)}) %collective-permute-start.12) | collective-permute-done | bytes 262176 | tf_op jit(solution)/shard_map/ppermute | solution.py:13
  136.3 7.1 %collective-permute-done.13 = bf16[16,8192]{1,0:T(8,128)(2,1)} collective-permute-done((bf16[16,8192]{1,0:T(8,128)(2,1)}, bf16[16,8192]{1,0:T(8,128)(2,1)}, u32[]{:S(2)}, u32[]{:S(2)}) %collective-permute-start.13) | collective-permute-done | bytes 262176 | tf_op jit(solution)/shard_map/ppermute | solution.py:13
  143.9 8.3 %collective-permute-done.14 = bf16[16,8192]{1,0:T(8,128)(2,1)} collective-permute-done((bf16[16,8192]{1,0:T(8,128)(2,1)}, bf16[16,8192]{1,0:T(8,128)(2,1)}, u32[]{:S(2)}, u32[]{:S(2)}) %collective-permute-start.14) | collective-permute-done | bytes 262176 | tf_op jit(solution)/shard_map/ppermute | solution.py:13
  153.2 1.0 constant_dynamic-update-slice_fusion.30
  154.1 1.0 constant_dynamic-update-slice_fusion.29
  156.4 1.0 constant_dynamic-update-slice_fusion.15
  160.7 2.2 %constant_dynamic-slice_fusion = bf16[256,8192]{1,0:T(8,128)(2,1)} fusion(bf16[512,8192]{1,0:T(8,128)(2,1)S(1)} %constant_dynamic-update-slice_fusion, s32[]{:T(128)S(6)} %select_n.28), kind=kLoop, calls=%fused_computation.73 | loop fusion | bytes 8388612 | tf_op jit(solution)/shard_map/jit(_roll_dynamic)/dynamic_slice | solution.py:16
  162.9 46.5 %while.18 = (s32[]{:T(128)}, f32[112]{0:T(128)S(1)}, f32[112]{0:T(128)S(1)}, bf16[256,8192]{1,0:T(8,128)(2,1)}, f32[16,16]{1,0:T(8,128)S(1)}, /*index=5*/f32[256...) while((s32[]{:T(128)}, f32[112]{0:T(128)S(1)}, ...), condition=%wide.region_7.8_spmd.clone, body=%wide.region_3.7_spmd.clone.sunk | while | flops 168249056 | bytes 2605173 | solution.py:72
  162.9 1.4 fusion.62
  164.3 1.2 custom-call.31
  166.0 2.1 %multiply_reduce_fusion.3 = (f32[1024]{0:T(1024)S(1)}, bf16[256,1024]{1,0:T(8,128)(2,1)S(1)}) fusion(f32[16,1024]{1,0:T(8,128)S(1)} %fusion.64, f32[256,16]{0,1:T(8,128)S(1)} %get-tuple-element.375, bf16[256,8192]{1,0:T(8,128)(2,1)} %get-tuple-element.373, s32[]{:T(128)S(6)} %select_n.34), kind=kOutput, calls=%fused_computation.5.clone.1 | convolution fusion | flops 51641344 | bytes 1134596 | tf_op jit(solution)/shard_map/while/body/eval_jaxpr/dot_general | solution.py:54
  168.7 1.4 fusion.62
  170.1 1.2 custom-call.31
  171.8 2.1 %multiply_reduce_fusion.3 = (f32[1024]{0:T(1024)S(1)}, bf16[256,1024]{1,0:T(8,128)(2,1)S(1)}) fusion(f32[16,1024]{1,0:T(8,128)S(1)} %fusion.64, f32[256,16]{0,1:T(8,128)S(1)} %get-tuple-element.375, bf16[256,8192]{1,0:T(8,128)(2,1)} %get-tuple-element.373, s32[]{:T(128)S(6)} %select_n.34), kind=kOutput, calls=%fused_computation.5.clone.1 | convolution fusion | flops 51641344 | bytes 1134596 | tf_op jit(solution)/shard_map/while/body/eval_jaxpr/dot_general | solution.py:54
  174.5 1.4 fusion.62
  175.9 1.2 custom-call.31
  177.6 2.1 %multiply_reduce_fusion.3 = (f32[1024]{0:T(1024)S(1)}, bf16[256,1024]{1,0:T(8,128)(2,1)S(1)}) fusion(f32[16,1024]{1,0:T(8,128)S(1)} %fusion.64, f32[256,16]{0,1:T(8,128)S(1)} %get-tuple-element.375, bf16[256,8192]{1,0:T(8,128)(2,1)} %get-tuple-element.373, s32[]{:T(128)S(6)} %select_n.34), kind=kOutput, calls=%fused_computation.5.clone.1 | convolution fusion | flops 51641344 | bytes 1134596 | tf_op jit(solution)/shard_map/while/body/eval_jaxpr/dot_general | solution.py:54
  180.3 1.4 fusion.62
  181.7 1.2 custom-call.31
  183.4 2.1 %multiply_reduce_fusion.3 = (f32[1024]{0:T(1024)S(1)}, bf16[256,1024]{1,0:T(8,128)(2,1)S(1)}) fusion(f32[16,1024]{1,0:T(8,128)S(1)} %fusion.64, f32[256,16]{0,1:T(8,128)S(1)} %get-tuple-element.375, bf16[256,8192]{1,0:T(8,128)(2,1)} %get-tuple-element.373, s32[]{:T(128)S(6)} %select_n.34), kind=kOutput, calls=%fused_computation.5.clone.1 | convolution fusion | flops 51641344 | bytes 1134596 | tf_op jit(solution)/shard_map/while/body/eval_jaxpr/dot_general | solution.py:54
  186.1 1.4 fusion.62
  187.5 1.2 custom-call.31
  189.2 2.1 %multiply_reduce_fusion.3 = (f32[1024]{0:T(1024)S(1)}, bf16[256,1024]{1,0:T(8,128)(2,1)S(1)}) fusion(f32[16,1024]{1,0:T(8,128)S(1)} %fusion.64, f32[256,16]{0,1:T(8,128)S(1)} %get-tuple-element.375, bf16[256,8192]{1,0:T(8,128)(2,1)} %get-tuple-element.373, s32[]{:T(128)S(6)} %select_n.34), kind=kOutput, calls=%fused_computation.5.clone.1 | convolution fusion | flops 51641344 | bytes 1134596 | tf_op jit(solution)/shard_map/while/body/eval_jaxpr/dot_general | solution.py:54
  192.0 1.4 fusion.62
  193.3 1.2 custom-call.31
  195.0 2.1 %multiply_reduce_fusion.3 = (f32[1024]{0:T(1024)S(1)}, bf16[256,1024]{1,0:T(8,128)(2,1)S(1)}) fusion(f32[16,1024]{1,0:T(8,128)S(1)} %fusion.64, f32[256,16]{0,1:T(8,128)S(1)} %get-tuple-element.375, bf16[256,8192]{1,0:T(8,128)(2,1)} %get-tuple-element.373, s32[]{:T(128)S(6)} %select_n.34), kind=kOutput, calls=%fused_computation.5.clone.1 | convolution fusion | flops 51641344 | bytes 1134596 | tf_op jit(solution)/shard_map/while/body/eval_jaxpr/dot_general | solution.py:54
  197.8 1.4 fusion.62
  199.2 1.2 custom-call.31
  200.9 2.1 %multiply_reduce_fusion.3 = (f32[1024]{0:T(1024)S(1)}, bf16[256,1024]{1,0:T(8,128)(2,1)S(1)}) fusion(f32[16,1024]{1,0:T(8,128)S(1)} %fusion.64, f32[256,16]{0,1:T(8,128)S(1)} %get-tuple-element.375, bf16[256,8192]{1,0:T(8,128)(2,1)} %get-tuple-element.373, s32[]{:T(128)S(6)} %select_n.34), kind=kOutput, calls=%fused_computation.5.clone.1 | convolution fusion | flops 51641344 | bytes 1134596 | tf_op jit(solution)/shard_map/while/body/eval_jaxpr/dot_general | solution.py:54
  203.6 1.4 fusion.62
  205.0 1.2 custom-call.31
  206.7 2.1 %multiply_reduce_fusion.3 = (f32[1024]{0:T(1024)S(1)}, bf16[256,1024]{1,0:T(8,128)(2,1)S(1)}) fusion(f32[16,1024]{1,0:T(8,128)S(1)} %fusion.64, f32[256,16]{0,1:T(8,128)S(1)} %get-tuple-element.375, bf16[256,8192]{1,0:T(8,128)(2,1)} %get-tuple-element.373, s32[]{:T(128)S(6)} %select_n.34), kind=kOutput, calls=%fused_computation.5.clone.1 | convolution fusion | flops 51641344 | bytes 1134596 | tf_op jit(solution)/shard_map/while/body/eval_jaxpr/dot_general | solution.py:54
  (118 shorter events, 20.2 us)
Async XLA Ops:
  0.6 155.8 %copy-start = (bf16[16,8192]{1,0:T(8,128)(2,1)S(1)}, bf16[16,8192]{1,0:T(8,128)(2,1)}, u32[]{:S(2)}) copy-start(bf16[16,8192]{1,0:T(8,128)(2,1)} %param.5) | copy-start | bytes 786436
  0.6 9.8 %collective-permute-start = (bf16[16,8192]{1,0:T(8,128)(2,1)}, bf16[16,8192]{1,0:T(8,128)(2,1)S(1)}, u32[]{:S(2)}, u32[]{:S(2)}) collective-permute-start(bf16[16,8192]{1,0:T(8,128)(2,1)} %param.5), channel_id=1, source_target_pairs={{0,1},{1,2},{2,3},{3,4},{4,5},{5,6},{6,7},{7,8},{8,9},{9,10},{10,1... | collective-permute-start | bytes 786440 | tf_op jit(solution)/shard_map/ppermute | solution.py:13
  10.4 8.5 %collective-permute-start.1 = (bf16[16,8192]{1,0:T(8,128)(2,1)S(1)}, bf16[16,8192]{1,0:T(8,128)(2,1)S(1)}, u32[]{:S(2)}, u32[]{:S(2)}) collective-permute-start(bf16[16,8192]{1,0:T(8,128)(2,1)S(1)} %collective-permute-done), channel_id=1, source_target_pairs={{0,1},{1,2},{2,3},{3,4},{4,5},{5,6},{6,7},{7,8},{8,9},{9,10},{10,1... | collective-permute-start | bytes 786440 | tf_op jit(solution)/shard_map/ppermute | solution.py:13
  18.9 8.5 %collective-permute-start.2 = (bf16[16,8192]{1,0:T(8,128)(2,1)S(1)}, bf16[16,8192]{1,0:T(8,128)(2,1)S(1)}, u32[]{:S(2)}, u32[]{:S(2)}) collective-permute-start(bf16[16,8192]{1,0:T(8,128)(2,1)S(1)} %collective-permute-done.1), channel_id=1, source_target_pairs={{0,1},{1,2},{2,3},{3,4},{4,5},{5,6},{6,7},{7,8},{8,9},{9,10},{10,1... | collective-permute-start | bytes 786440 | tf_op jit(solution)/shard_map/ppermute | solution.py:13
  27.4 8.5 %collective-permute-start.3 = (bf16[16,8192]{1,0:T(8,128)(2,1)S(1)}, bf16[16,8192]{1,0:T(8,128)(2,1)S(1)}, u32[]{:S(2)}, u32[]{:S(2)}) collective-permute-start(bf16[16,8192]{1,0:T(8,128)(2,1)S(1)} %collective-permute-done.2), channel_id=1, source_target_pairs={{0,1},{1,2},{2,3},{3,4},{4,5},{5,6},{6,7},{7,8},{8,9},{9,10},{10,1... | collective-permute-start | bytes 786440 | tf_op jit(solution)/shard_map/ppermute | solution.py:13
  35.9 8.5 %collective-permute-start.4 = (bf16[16,8192]{1,0:T(8,128)(2,1)S(1)}, bf16[16,8192]{1,0:T(8,128)(2,1)S(1)}, u32[]{:S(2)}, u32[]{:S(2)}) collective-permute-start(bf16[16,8192]{1,0:T(8,128)(2,1)S(1)} %collective-permute-done.3), channel_id=1, source_target_pairs={{0,1},{1,2},{2,3},{3,4},{4,5},{5,6},{6,7},{7,8},{8,9},{9,10},{10,1... | collective-permute-start | bytes 786440 | tf_op jit(solution)/shard_map/ppermute | solution.py:13
  44.4 8.5 %collective-permute-start.5 = (bf16[16,8192]{1,0:T(8,128)(2,1)S(1)}, bf16[16,8192]{1,0:T(8,128)(2,1)S(1)}, u32[]{:S(2)}, u32[]{:S(2)}) collective-permute-start(bf16[16,8192]{1,0:T(8,128)(2,1)S(1)} %collective-permute-done.4), channel_id=1, source_target_pairs={{0,1},{1,2},{2,3},{3,4},{4,5},{5,6},{6,7},{7,8},{8,9},{9,10},{10,1... | collective-permute-start | bytes 786440 | tf_op jit(solution)/shard_map/ppermute | solution.py:13
  52.9 8.5 %collective-permute-start.6 = (bf16[16,8192]{1,0:T(8,128)(2,1)S(1)}, bf16[16,8192]{1,0:T(8,128)(2,1)S(1)}, u32[]{:S(2)}, u32[]{:S(2)}) collective-permute-start(bf16[16,8192]{1,0:T(8,128)(2,1)S(1)} %collective-permute-done.5), channel_id=1, source_target_pairs={{0,1},{1,2},{2,3},{3,4},{4,5},{5,6},{6,7},{7,8},{8,9},{9,10},{10,1... | collective-permute-start | bytes 786440 | tf_op jit(solution)/shard_map/ppermute | solution.py:13
  61.4 8.5 %collective-permute-start.7 = (bf16[16,8192]{1,0:T(8,128)(2,1)S(1)}, bf16[16,8192]{1,0:T(8,128)(2,1)S(1)}, u32[]{:S(2)}, u32[]{:S(2)}) collective-permute-start(bf16[16,8192]{1,0:T(8,128)(2,1)S(1)} %collective-permute-done.6), channel_id=1, source_target_pairs={{0,1},{1,2},{2,3},{3,4},{4,5},{5,6},{6,7},{7,8},{8,9},{9,10},{10,1... | collective-permute-start | bytes 786440 | tf_op jit(solution)/shard_map/ppermute | solution.py:13
  69.9 8.5 %collective-permute-start.8 = (bf16[16,8192]{1,0:T(8,128)(2,1)S(1)}, bf16[16,8192]{1,0:T(8,128)(2,1)S(1)}, u32[]{:S(2)}, u32[]{:S(2)}) collective-permute-start(bf16[16,8192]{1,0:T(8,128)(2,1)S(1)} %collective-permute-done.7), channel_id=1, source_target_pairs={{0,1},{1,2},{2,3},{3,4},{4,5},{5,6},{6,7},{7,8},{8,9},{9,10},{10,1... | collective-permute-start | bytes 786440 | tf_op jit(solution)/shard_map/ppermute | solution.py:13
  78.4 8.5 %collective-permute-start.9 = (bf16[16,8192]{1,0:T(8,128)(2,1)S(1)}, bf16[16,8192]{1,0:T(8,128)(2,1)S(1)}, u32[]{:S(2)}, u32[]{:S(2)}) collective-permute-start(bf16[16,8192]{1,0:T(8,128)(2,1)S(1)} %collective-permute-done.8), channel_id=1, source_target_pairs={{0,1},{1,2},{2,3},{3,4},{4,5},{5,6},{6,7},{7,8},{8,9},{9,10},{10,1... | collective-permute-start | bytes 786440 | tf_op jit(solution)/shard_map/ppermute | solution.py:13
  86.9 30.2 %collective-permute-start.10 = (bf16[16,8192]{1,0:T(8,128)(2,1)S(1)}, bf16[16,8192]{1,0:T(8,128)(2,1)S(1)}, u32[]{:S(2)}, u32[]{:S(2)}) collective-permute-start(bf16[16,8192]{1,0:T(8,128)(2,1)S(1)} %collective-permute-done.9), channel_id=1, source_target_pairs={{0,1},{1,2},{2,3},{3,4},{4,5},{5,6},{6,7},{7,8},{8,9},{9,10},{10,1... | collective-permute-start | bytes 786440 | tf_op jit(solution)/shard_map/ppermute | solution.py:13
  88.6 39.1 %all-to-all-start = ((f32[16,16,112]{2,0,1:T(8,128)}), f32[16,16,112]{2,0,1:T(8,128)S(1)}, u32[]{:S(2)}, u32[]{:S(2)}) async-start(f32[16,16,112]{2,0,1:T(8,128)} %copy.15), calls=%async_computation | async-start | bytes 262144 | tf_op jit(solution)/shard_map/all_to_all | solution.py:31
  117.1 8.6 %collective-permute-start.11 = (bf16[16,8192]{1,0:T(8,128)(2,1)S(1)}, bf16[16,8192]{1,0:T(8,128)(2,1)}, u32[]{:S(2)}, u32[]{:S(2)}) collective-permute-start(bf16[16,8192]{1,0:T(8,128)(2,1)S(1)} %collective-permute-done.10), channel_id=1, source_target_pairs={{0,1},{1,2},{2,3},{3,4},{4,5},{5,6},{6,7},{7,8},{8,9},{9,10},{10,1... | collective-permute-start | bytes 786440 | tf_op jit(solution)/shard_map/ppermute | solution.py:13
  125.8 8.8 %collective-permute-start.12 = (bf16[16,8192]{1,0:T(8,128)(2,1)}, bf16[16,8192]{1,0:T(8,128)(2,1)}, u32[]{:S(2)}, u32[]{:S(2)}) collective-permute-start(bf16[16,8192]{1,0:T(8,128)(2,1)} %collective-permute-done.11), channel_id=1, source_target_pairs={{0,1},{1,2},{2,3},{3,4},{4,5},{5,6},{6,7},{7,8},{8,9},{9,10},{10,1... | collective-permute-start | bytes 786440 | tf_op jit(solution)/shard_map/ppermute | solution.py:13
  134.6 8.8 %collective-permute-start.13 = (bf16[16,8192]{1,0:T(8,128)(2,1)}, bf16[16,8192]{1,0:T(8,128)(2,1)}, u32[]{:S(2)}, u32[]{:S(2)}) collective-permute-start(bf16[16,8192]{1,0:T(8,128)(2,1)} %collective-permute-done.12), channel_id=1, source_target_pairs={{0,1},{1,2},{2,3},{3,4},{4,5},{5,6},{6,7},{7,8},{8,9},{9,10},{10,1... | collective-permute-start | bytes 786440 | tf_op jit(solution)/shard_map/ppermute | solution.py:13
  143.4 8.8 %collective-permute-start.14 = (bf16[16,8192]{1,0:T(8,128)(2,1)}, bf16[16,8192]{1,0:T(8,128)(2,1)}, u32[]{:S(2)}, u32[]{:S(2)}) collective-permute-start(bf16[16,8192]{1,0:T(8,128)(2,1)} %collective-permute-done.13), channel_id=1, source_target_pairs={{0,1},{1,2},{2,3},{3,4},{4,5},{5,6},{6,7},{7,8},{8,9},{9,10},{10,1... | collective-permute-start | bytes 786440 | tf_op jit(solution)/shard_map/ppermute | solution.py:13
  156.4 6.5 %copy-start.1 = (f32[112]{0:T(128)S(1)}, f32[112]{0:T(128)}, u32[]{:S(2)}) copy-start(f32[112]{0:T(128)} %custom-call.25) | copy-start | bytes 1348
  156.4 6.5 %copy-start.2 = (f32[112]{0:T(128)S(1)}, f32[112]{0:T(128)}, u32[]{:S(2)}) copy-start(f32[112]{0:T(128)} %custom-call.26) | copy-start | bytes 1348
